TPU v7x, 32 devices: a whole 2x2x4 slice. The times are simulated.
32 devices in a mesh: groups: 2 (over y), section: 4 (over z), seq: 4 (over x, core).
Axes of the slice: x: 2, y: 2, z: 4, core: 2. Of those that a mesh axis runs over, the one named last changes fastest.
Arguments:
- tokens: bfloat16 [8, 256, 1440], P('groups', 'seq'), parts along dimension 0, may hold values from -6 to 6
- block_order: int32 [8], P('groups'), parts along dimension 0, may hold values from 0 to 3, each once
- prompt_lengths: int32 [8], P('groups'), parts along dimension 0, may hold values from 1 to 256, 576 in all
- norm_gain: float32 [4, 1440], P('section'), may hold values from 0.1 to 1.9
- w_query: bfloat16 [4, 1440, 2048], P('section', None, 'seq'), may hold values from -4 to 4
- w_key_value: bfloat16 [4, 1440, 512], P('section'), may hold values from -4 to 4
- w_out: bfloat16 [4, 2048, 1440], P('section', 'seq'), may hold values from -0.125 to 0.125
- sink_logits: float32 [4, 32], P('section'), may hold values from 0 to 4
Outputs:
- hidden_states: bfloat16 [4, 8, 256, 1440], P('section', 'groups', 'seq'), parts along dimension 1
- layer_cache: bfloat16 [4, 8, 256, 512], P('section', 'groups', 'seq'), parts along dimension 1
There are 2 independent parts, one for each index of `groups`. A program takes and returns all parts, laid end to end along the dimension named above; an argument that names none is the same for every part. Nothing has to cross between parts.
Inputs may be any that keep to these rules, and one draw needn't show every extreme that they name: `block_order`: each of 0 to 3 exactly once. `prompt_lengths`: the longest prompt is full.
All inputs are finite; a program needn't handle non-finite values.
Results may differ from a plain program's by a relative error of at most 0.024.
Values may be sent and summed in bfloat16 or wider, within the bound.
A program may use at most 128 MiB of HBM per device.

v0:
```python
import math

import jax
import jax.numpy as jnp
from jax import lax
from jax.sharding import PartitionSpec as P

HEAD_DIM = 64
WIN = 128


THETA = 150000.0
EPSILON = 1e-05


def from_behind(block, axis, distance):
    devices = range(lax.axis_size(axis))
    route = [(i - distance, i) for i in devices if i - distance in devices]
    return lax.ppermute(block, axis, route)


def rotary(positions, head_size):
    half = head_size // 2
    freq = jnp.exp(jnp.arange(half, dtype=jnp.float32) * (-2.0 * math.log(THETA) / head_size))
    angles = positions.astype(jnp.float32)[:, None] * freq[None, :]
    return (jnp.cos(angles)[:, None, :], jnp.sin(angles)[:, None, :])


def rotate(values, cosine, sine):
    half = values.shape[-1] // 2
    first = values[..., :half]
    second = values[..., half:]
    return jnp.concatenate([first * cosine - second * sine, second * cosine + first * sine], -1)


def per_device(
    tokens, block_order, prompt_lengths, norm_gain, w_query, w_key_value, w_out, sink_logits
):
    section_index = lax.axis_index("section")
    sections = lax.axis_size("section")
    seq_index = lax.axis_index("seq")
    micro, rows, width = tokens.shape
    full_query, full_out = (
        lax.all_gather(w_query, "seq", axis=2, tiled=True),
        lax.all_gather(w_out, "seq", axis=1, tiled=True),
    )
    query_weight = full_query[0]
    out_weight = full_out[0]
    pair_weight = w_key_value[0]
    gain = norm_gain[0]
    heads_width = query_weight.shape[1]
    head_count = heads_width // HEAD_DIM
    kv_width = pair_weight.shape[1] // 2
    kv_heads = kv_width // HEAD_DIM
    group = head_count // kv_heads
    sink = sink_logits[0].reshape(kv_heads, group)[:, :, None]
    keep = min(WIN, rows)
    depth = WIN // keep
    start = seq_index * rows
    positions = start + jnp.arange(rows, dtype=jnp.int32)
    cosine, sine = rotary(positions, HEAD_DIM)
    key_positions = start - WIN + jnp.arange(WIN + rows, dtype=jnp.int32)

    def project(hidden):
        widened = hidden.astype(jnp.float32)
        scale = lax.rsqrt(jnp.mean(widened * widened, -1, keepdims=True) + EPSILON)
        normed = (widened * scale * gain).astype(jnp.bfloat16)
        queries = jnp.dot(normed, query_weight, preferred_element_type=jnp.float32).reshape(
            rows, head_count, HEAD_DIM
        )
        queries = rotate(queries, cosine, sine).astype(jnp.bfloat16).reshape(rows, heads_width)
        projected = jnp.dot(normed, pair_weight, preferred_element_type=jnp.float32)
        rotated = rotate(
            projected[:, :kv_width].reshape(rows, kv_heads, HEAD_DIM), cosine, sine
        ).reshape(rows, kv_width)
        cache = jnp.concatenate([rotated, projected[:, kv_width:]], 1).astype(jnp.bfloat16)
        return (queries, cache)

    def project_spare(hidden):
        return (
            jnp.zeros((rows, heads_width), jnp.bfloat16),
            jnp.zeros((rows, 2 * kv_width), jnp.bfloat16),
        )

    def window_of(cache):
        pieces = [from_behind(cache, "seq", offset) for offset in range(depth, 0, -1)]
        return jnp.concatenate(pieces, 0)

    def attend(operands):
        hidden, queries, cache, window, length = operands
        joined = jnp.concatenate([window, cache], 0)
        key_heads = joined[:, :kv_width].reshape(WIN + rows, kv_heads, HEAD_DIM)
        value_heads = joined[:, kv_width:].reshape(WIN + rows, kv_heads, HEAD_DIM)
        grouped = queries.reshape(rows, kv_heads, group, HEAD_DIM)
        scores = (
            jnp.einsum("qkgd,skd->kgqs", grouped, key_heads, preferred_element_type=jnp.float32)
            * 0.125
        )
        query_col = positions[:, None]
        key_row = key_positions[None, :]
        allowed = (key_row <= query_col) & (query_col - key_row < WIN) & (key_row >= 0)
        allowed = allowed & ((key_row < length) | (key_row == query_col))
        masked = jnp.where(allowed, scores, jnp.float32(-1e30))
        top = jnp.maximum(jnp.max(masked, -1), sink)
        expo = jnp.where(allowed, jnp.exp(scores - top[..., None]), jnp.float32(0.0))
        total = jnp.sum(expo, -1) + jnp.exp(sink - top)
        weights = (expo / total[..., None]).astype(jnp.bfloat16)
        context = jnp.einsum(
            "kgqs,skd->qkgd", weights, value_heads, preferred_element_type=jnp.float32
        )
        context = context.reshape(rows, heads_width).astype(jnp.bfloat16)
        output = jnp.dot(context, out_weight, preferred_element_type=jnp.float32)
        return (hidden.astype(jnp.float32) + output).astype(jnp.bfloat16)

    def pass_through(operands):
        return operands[0]

    def turn(counter, carry):
        arriving, hidden_buffer, cache_buffer = carry
        slot = counter - section_index
        active = (slot >= 0) & (slot < micro)
        slot_safe = jnp.clip(slot, 0, micro - 1)
        block = block_order[slot_safe]
        length = prompt_lengths[block]
        entering = lax.dynamic_index_in_dim(tokens, block, 0, keepdims=False)
        hidden = jnp.where(section_index == 0, entering, arriving)
        queries, cache = lax.cond(active, project, project_spare, hidden)
        window = window_of(cache)
        updated = lax.cond(active, attend, pass_through, (hidden, queries, cache, window, length))
        previous_hidden = lax.dynamic_index_in_dim(hidden_buffer, slot_safe, 0, keepdims=False)
        previous_cache = lax.dynamic_index_in_dim(cache_buffer, slot_safe, 0, keepdims=False)
        hidden_buffer = lax.dynamic_update_index_in_dim(
            hidden_buffer, jnp.where(active, updated, previous_hidden), slot_safe, 0
        )
        cache_buffer = lax.dynamic_update_index_in_dim(
            cache_buffer, jnp.where(active, cache, previous_cache), slot_safe, 0
        )
        passed = from_behind(updated, "section", 1)
        return (passed, hidden_buffer, cache_buffer)

    initial = (
        jnp.zeros((rows, width), jnp.bfloat16),
        jnp.zeros((micro, rows, width), jnp.bfloat16),
        jnp.zeros((micro, rows, 2 * kv_width), jnp.bfloat16),
    )
    final = lax.fori_loop(0, micro + sections - 1, turn, initial)
    return (final[1][None], final[2][None])


def solution(mesh):
    in_specs = (
        P("groups", "seq", None),
        P("groups"),
        P("groups"),
        P("section", None),
        P("section", None, "seq"),
        P("section", None, None),
        P("section", "seq", None),
        P("section", None),
    )
    out_specs = (P("section", "groups", "seq", None), P("section", "groups", "seq", None))
    return jax.shard_map(
        per_device, mesh=mesh, in_specs=in_specs, out_specs=out_specs, check_vma=False
    )
```

profile of v0, /device:TPU:28, one launch (start us, length us, event | category | flops | bytes accessed | tf_op | source)
XLA Modules:
  0.0 363.9 jit_solution(2830805438816558788)
XLA Ops:
  8.5 1.6 copy.14
  11.5 43.2 %all-gather.3.cloned.1.call-done = bf16[1,1440,2048]{2,1,0:T(8,128)(2,1)} async-done(((bf16[1,1440,512]{2,1,0:T(8,128)(2,1)}), bf16[1,1440,2048]{2,1,0:T(8,128)(2,1)}) %all-gather.3.cloned.1.call-update) | async-done | bytes 5898256 | tf_op jit(solution)/shard_map/all_gather | solution.py:44
  54.6 47.9 %all-gather.5.cloned.1.call-done = bf16[1,2048,1440]{2,1,0:T(8,128)(2,1)} async-done(((bf16[1,512,1440]{2,1,0:T(8,128)(2,1)}), bf16[1,2048,1440]{2,1,0:T(8,128)(2,1)}) %all-gather.5.cloned.1.call-update) | async-done | bytes 5898256 | tf_op jit(solution)/shard_map/all_gather | solution.py:45
  104.3 252.8 %while.20 = (s32[]{:T(128)}, bf16[64,1440]{1,0:T(8,128)(2,1)S(1)}, bf16[4,64,1440]{2,1,0:T(8,128)(2,1)}, bf16[4,64,512]{2,1,0:T(8,128)(2,1)}, s32[]{:T(128)}, /*...) while((s32[]{:T(128)}, bf16[64,1440]{1,0:T(8,128)(2,1)S(1)}, ...), condition=%wide.region_8.9_spmd.clone.clone, body=%wide.region_0.8_spmd.clone.clone.sunk | while | flops 958372544 | bytes 47880768 | solution.py:146
  107.8 1.4 conditional.8
  109.1 2.5 collective-permute-start
  111.6 1.9 collective-permute-start.1
  118.0 7.3 %collective-permute-done.2 = bf16[64,1440]{1,0:T(8,128)(2,1)S(1)} collective-permute-done((bf16[64,1440]{1,0:T(8,128)(2,1)S(1)}, bf16[64,1440]{1,0:T(8,128)(2,1)S(1)}, u32[]{:S(2)}, u32[]{:S(2)}) %collective-permute-start.2) | collective-permute-done | bytes 184352 | tf_op jit(solution)/shard_map/while/body/eval_jaxpr/ppermute | solution.py:19
  128.8 1.4 conditional.8
  130.1 3.0 collective-permute-start
  133.2 1.3 collective-permute-start.1
  139.0 7.2 %collective-permute-done.2 = bf16[64,1440]{1,0:T(8,128)(2,1)S(1)} collective-permute-done((bf16[64,1440]{1,0:T(8,128)(2,1)S(1)}, bf16[64,1440]{1,0:T(8,128)(2,1)S(1)}, u32[]{:S(2)}, u32[]{:S(2)}) %collective-permute-start.2) | collective-permute-done | bytes 184352 | tf_op jit(solution)/shard_map/while/body/eval_jaxpr/ppermute | solution.py:19
  149.6 1.4 conditional.8
  151.0 3.0 collective-permute-start
  154.0 1.3 collective-permute-start.1
  159.8 50.5 %collective-permute-done.2 = bf16[64,1440]{1,0:T(8,128)(2,1)S(1)} collective-permute-done((bf16[64,1440]{1,0:T(8,128)(2,1)S(1)}, bf16[64,1440]{1,0:T(8,128)(2,1)S(1)}, u32[]{:S(2)}, u32[]{:S(2)}) %collective-permute-start.2) | collective-permute-done | bytes 184352 | tf_op jit(solution)/shard_map/while/body/eval_jaxpr/ppermute | solution.py:19
  213.8 9.2 %conditional.8 = (bf16[64,2048]{1,0:T(8,128)(2,1)S(1)}, bf16[64,512]{1,0:T(8,128)(2,1)}, bf16[64,512]{0,1:T(8,128)(2,1)}) conditional(s32[]{:T(128)} %convert_element_type.69, () %tuple.79, (bf16[64,1440]{1,0:T(8,128)(2,1)S(1)}, f32[1,1440]{1,0:T(1,128)S(1)}, bf16[1440,2048]{1,0:T(8,128)(2,1)}, f32[64,1,32]{2,0,1:T(8,128)S(1)}, ...), branch_computations={%region_1.1_spmd, %region_2.3_spmd} | conditional | flops 474183744 | bytes 12373788 | solution.py:127
  214.0 3.9 %fusion.26 = f32[64,2048]{1,0:T(8,128)S(1)} fusion(bf16[1440,2048]{1,0:T(8,128)(2,1)} %get-tuple-element.374, bf16[64,1440]{1,0:T(8,128)(2,1)S(1)} %get-tuple-element.372, f32[1440]{0:T(1024)S(1)} %reduce, f32[64]{0:T(128)S(1)} %add_rsqrt_fusion), kind=kOutput, calls=%fused_computation.44 | convolution fusion | flops 377856000 | bytes 6612864 | tf_op jit(solution)/shard_map/while/body/eval_jaxpr/cond/branch_1_fun/dot_general | solution.py:68
  221.4 1.6 copy.18
  223.0 2.3 collective-permute-start
  225.4 1.3 collective-permute-start.1
  228.5 1.5 bitcast_dynamic-update-slice_fusion.5
  230.0 8.0 %conditional.9 = (bf16[64,1440]{1,0:T(8,128)(2,1)S(1)}) conditional(s32[]{:T(128)} %convert_element_type.69, bf16[64,1440]{1,0:T(8,128)(2,1)S(1)} %bitcast_select_fusion.5, (bf16[64,1440]{1,0:T(8,128)(2,1)S(1)}, bf16[64,512]{0,1:T(8,128)(2,1)S(1)}, bf16[64,512]{0,1:T(8,128)(2,1)S(1)}, bf16[64,512]{1,0:T(8,128)(2,1)}, s32[]{:T(128)}, ...), branch_computations={%region_4.4_spmd, %region_5.7_spmd} | conditional | flops 483969664 | bytes 32420688 | solution.py:129
  240.0 7.1 %collective-permute-done.2 = bf16[64,1440]{1,0:T(8,128)(2,1)S(1)} collective-permute-done((bf16[64,1440]{1,0:T(8,128)(2,1)S(1)}, bf16[64,1440]{1,0:T(8,128)(2,1)S(1)}, u32[]{:S(2)}, u32[]{:S(2)}) %collective-permute-start.2) | collective-permute-done | bytes 184352 | tf_op jit(solution)/shard_map/while/body/eval_jaxpr/ppermute | solution.py:19
  250.6 9.2 %conditional.8 = (bf16[64,2048]{1,0:T(8,128)(2,1)S(1)}, bf16[64,512]{1,0:T(8,128)(2,1)}, bf16[64,512]{0,1:T(8,128)(2,1)}) conditional(s32[]{:T(128)} %convert_element_type.69, () %tuple.79, (bf16[64,1440]{1,0:T(8,128)(2,1)S(1)}, f32[1,1440]{1,0:T(1,128)S(1)}, bf16[1440,2048]{1,0:T(8,128)(2,1)}, f32[64,1,32]{2,0,1:T(8,128)S(1)}, ...), branch_computations={%region_1.1_spmd, %region_2.3_spmd} | conditional | flops 474183744 | bytes 12373788 | solution.py:127
  250.8 3.9 %fusion.26 = f32[64,2048]{1,0:T(8,128)S(1)} fusion(bf16[1440,2048]{1,0:T(8,128)(2,1)} %get-tuple-element.374, bf16[64,1440]{1,0:T(8,128)(2,1)S(1)} %get-tuple-element.372, f32[1440]{0:T(1024)S(1)} %reduce, f32[64]{0:T(128)S(1)} %add_rsqrt_fusion), kind=kOutput, calls=%fused_computation.44 | convolution fusion | flops 377856000 | bytes 6612864 | tf_op jit(solution)/shard_map/while/body/eval_jaxpr/cond/branch_1_fun/dot_general | solution.py:68
  258.2 1.6 copy.18
  259.8 2.3 collective-permute-start
  262.1 1.3 collective-permute-start.1
  265.2 1.5 bitcast_dynamic-update-slice_fusion.5
  266.7 8.0 %conditional.9 = (bf16[64,1440]{1,0:T(8,128)(2,1)S(1)}) conditional(s32[]{:T(128)} %convert_element_type.69, bf16[64,1440]{1,0:T(8,128)(2,1)S(1)} %bitcast_select_fusion.5, (bf16[64,1440]{1,0:T(8,128)(2,1)S(1)}, bf16[64,512]{0,1:T(8,128)(2,1)S(1)}, bf16[64,512]{0,1:T(8,128)(2,1)S(1)}, bf16[64,512]{1,0:T(8,128)(2,1)}, s32[]{:T(128)}, ...), branch_computations={%region_4.4_spmd, %region_5.7_spmd} | conditional | flops 483969664 | bytes 32420688 | solution.py:129
  276.8 7.1 %collective-permute-done.2 = bf16[64,1440]{1,0:T(8,128)(2,1)S(1)} collective-permute-done((bf16[64,1440]{1,0:T(8,128)(2,1)S(1)}, bf16[64,1440]{1,0:T(8,128)(2,1)S(1)}, u32[]{:S(2)}, u32[]{:S(2)}) %collective-permute-start.2) | collective-permute-done | bytes 184352 | tf_op jit(solution)/shard_map/while/body/eval_jaxpr/ppermute | solution.py:19
  287.3 9.2 %conditional.8 = (bf16[64,2048]{1,0:T(8,128)(2,1)S(1)}, bf16[64,512]{1,0:T(8,128)(2,1)}, bf16[64,512]{0,1:T(8,128)(2,1)}) conditional(s32[]{:T(128)} %convert_element_type.69, () %tuple.79, (bf16[64,1440]{1,0:T(8,128)(2,1)S(1)}, f32[1,1440]{1,0:T(1,128)S(1)}, bf16[1440,2048]{1,0:T(8,128)(2,1)}, f32[64,1,32]{2,0,1:T(8,128)S(1)}, ...), branch_computations={%region_1.1_spmd, %region_2.3_spmd} | conditional | flops 474183744 | bytes 12373788 | solution.py:127
  287.5 3.9 %fusion.26 = f32[64,2048]{1,0:T(8,128)S(1)} fusion(bf16[1440,2048]{1,0:T(8,128)(2,1)} %get-tuple-element.374, bf16[64,1440]{1,0:T(8,128)(2,1)S(1)} %get-tuple-element.372, f32[1440]{0:T(1024)S(1)} %reduce, f32[64]{0:T(128)S(1)} %add_rsqrt_fusion), kind=kOutput, calls=%fused_computation.44 | convolution fusion | flops 377856000 | bytes 6612864 | tf_op jit(solution)/shard_map/while/body/eval_jaxpr/cond/branch_1_fun/dot_general | solution.py:68
  294.9 1.6 copy.18
  296.5 2.3 collective-permute-start
  298.9 1.3 collective-permute-start.1
  302.0 1.5 bitcast_dynamic-update-slice_fusion.5
  303.5 8.0 %conditional.9 = (bf16[64,1440]{1,0:T(8,128)(2,1)S(1)}) conditional(s32[]{:T(128)} %convert_element_type.69, bf16[64,1440]{1,0:T(8,128)(2,1)S(1)} %bitcast_select_fusion.5, (bf16[64,1440]{1,0:T(8,128)(2,1)S(1)}, bf16[64,512]{0,1:T(8,128)(2,1)S(1)}, bf16[64,512]{0,1:T(8,128)(2,1)S(1)}, bf16[64,512]{1,0:T(8,128)(2,1)}, s32[]{:T(128)}, ...), branch_computations={%region_4.4_spmd, %region_5.7_spmd} | conditional | flops 483969664 | bytes 32420688 | solution.py:129
  313.5 7.1 %collective-permute-done.2 = bf16[64,1440]{1,0:T(8,128)(2,1)S(1)} collective-permute-done((bf16[64,1440]{1,0:T(8,128)(2,1)S(1)}, bf16[64,1440]{1,0:T(8,128)(2,1)S(1)}, u32[]{:S(2)}, u32[]{:S(2)}) %collective-permute-start.2) | collective-permute-done | bytes 184352 | tf_op jit(solution)/shard_map/while/body/eval_jaxpr/ppermute | solution.py:19
  324.1 9.2 %conditional.8 = (bf16[64,2048]{1,0:T(8,128)(2,1)S(1)}, bf16[64,512]{1,0:T(8,128)(2,1)}, bf16[64,512]{0,1:T(8,128)(2,1)}) conditional(s32[]{:T(128)} %convert_element_type.69, () %tuple.79, (bf16[64,1440]{1,0:T(8,128)(2,1)S(1)}, f32[1,1440]{1,0:T(1,128)S(1)}, bf16[1440,2048]{1,0:T(8,128)(2,1)}, f32[64,1,32]{2,0,1:T(8,128)S(1)}, ...), branch_computations={%region_1.1_spmd, %region_2.3_spmd} | conditional | flops 474183744 | bytes 12373788 | solution.py:127
  324.3 3.9 %fusion.26 = f32[64,2048]{1,0:T(8,128)S(1)} fusion(bf16[1440,2048]{1,0:T(8,128)(2,1)} %get-tuple-element.374, bf16[64,1440]{1,0:T(8,128)(2,1)S(1)} %get-tuple-element.372, f32[1440]{0:T(1024)S(1)} %reduce, f32[64]{0:T(128)S(1)} %add_rsqrt_fusion), kind=kOutput, calls=%fused_computation.44 | convolution fusion | flops 377856000 | bytes 6612864 | tf_op jit(solution)/shard_map/while/body/eval_jaxpr/cond/branch_1_fun/dot_general | solution.py:68
  331.7 1.6 copy.18
  333.3 2.3 collective-permute-start
  335.6 1.3 collective-permute-start.1
  338.7 1.5 bitcast_dynamic-update-slice_fusion.5
  340.2 8.0 %conditional.9 = (bf16[64,1440]{1,0:T(8,128)(2,1)S(1)}) conditional(s32[]{:T(128)} %convert_element_type.69, bf16[64,1440]{1,0:T(8,128)(2,1)S(1)} %bitcast_select_fusion.5, (bf16[64,1440]{1,0:T(8,128)(2,1)S(1)}, bf16[64,512]{0,1:T(8,128)(2,1)S(1)}, bf16[64,512]{0,1:T(8,128)(2,1)S(1)}, bf16[64,512]{1,0:T(8,128)(2,1)}, s32[]{:T(128)}, ...), branch_computations={%region_4.4_spmd, %region_5.7_spmd} | conditional | flops 483969664 | bytes 32420688 | solution.py:129
  350.3 6.8 %collective-permute-done.2 = bf16[64,1440]{1,0:T(8,128)(2,1)S(1)} collective-permute-done((bf16[64,1440]{1,0:T(8,128)(2,1)S(1)}, bf16[64,1440]{1,0:T(8,128)(2,1)S(1)}, u32[]{:S(2)}, u32[]{:S(2)}) %collective-permute-start.2) | collective-permute-done | bytes 184352 | tf_op jit(solution)/shard_map/while/body/eval_jaxpr/ppermute | solution.py:19
  (260 shorter events, 94.6 us)
Async XLA Ops:
  7.2 1.4 copy-start.1
  7.2 47.5 %all-gather.3.cloned.1.call-start = ((), (), s32[]{:S(2)}) async-start(), calls=%async_computation | async-start | bytes 7372800 | tf_op jit(solution)/shard_map/all_gather | solution.py:44
  7.9 2.8 copy-start.3
  7.9 94.7 %all-gather.5.cloned.1.call-start = ((), (), s32[]{:S(2)}) async-start(), calls=%async_computation.1 | async-start | bytes 7864320 | tf_op jit(solution)/shard_map/all_gather | solution.py:45
  10.2 94.1 %copy-start = (bf16[1,1440,512]{2,1,0:T(8,128)(2,1)S(1)}, bf16[1,1440,512]{2,1,0:T(8,128)(2,1)}, u32[]{:S(2)}) copy-start(bf16[1,1440,512]{2,1,0:T(8,128)(2,1)} %param.19) | copy-start | bytes 4423684
  10.2 94.1 %copy-start.2 = (f32[1,1440]{1,0:T(1,128)S(1)}, f32[1,1440]{1,0:T(1,128)}, u32[]{:S(2)}) copy-start(f32[1,1440]{1,0:T(1,128)} %param.17) | copy-start | bytes 17284
  10.2 94.1 %copy-start.4 = (s32[4]{0:T(128)S(1)}, s32[4]{0:T(128)}, u32[]{:S(2)}) copy-start(s32[4]{0:T(128)} %param.15) | copy-start | bytes 52
  10.2 94.1 %copy-start.5 = (s32[4]{0:T(128)S(1)}, s32[4]{0:T(128)}, u32[]{:S(2)}) copy-start(s32[4]{0:T(128)} %param.16) | copy-start | bytes 52
  109.1 6.8 %collective-permute-start = (bf16[64,512]{0,1:T(8,128)(2,1)}, bf16[64,512]{0,1:T(8,128)(2,1)S(1)}, u32[]{:S(2)}, u32[]{:S(2)}) collective-permute-start(bf16[64,512]{0,1:T(8,128)(2,1)} %get-tuple-element.696), channel_id=1, source_target_pairs={{0,2},{1,3},{4,6},{5,7},{8,10},{9,11},{12,14},{13,15},{16,18},{17,... | collective-permute-start | bytes 196616 | tf_op jit(solution)/shard_map/while/body/eval_jaxpr/ppermute | solution.py:19
  111.6 4.3 %collective-permute-start.1 = (bf16[64,512]{0,1:T(8,128)(2,1)}, bf16[64,512]{0,1:T(8,128)(2,1)S(1)}, u32[]{:S(2)}, u32[]{:S(2)}) collective-permute-start(bf16[64,512]{0,1:T(8,128)(2,1)} %get-tuple-element.696), channel_id=1, source_target_pairs={{0,1},{1,2},{2,3},{4,5},{5,6},{6,7},{8,9},{9,10},{10,11},{12,13},{... | collective-permute-start | bytes 196616 | tf_op jit(solution)/shard_map/while/body/eval_jaxpr/ppermute | solution.py:19
  116.0 9.3 %collective-permute-start.2 = (bf16[64,1440]{1,0:T(8,128)(2,1)S(1)}, bf16[64,1440]{1,0:T(8,128)(2,1)S(1)}, u32[]{:S(2)}, u32[]{:S(2)}) collective-permute-start(bf16[64,1440]{1,0:T(8,128)(2,1)S(1)} %get-tuple-element.771), channel_id=1, source_target_pairs={{0,4},{4,8},{8,12},{1,5},{5,9},{9,13},{2,6},{6,10},{10,14},{3,7},{... | collective-permute-start | bytes 552968 | tf_op jit(solution)/shard_map/while/body/eval_jaxpr/ppermute | solution.py:19
  130.1 6.8 %collective-permute-start = (bf16[64,512]{0,1:T(8,128)(2,1)}, bf16[64,512]{0,1:T(8,128)(2,1)S(1)}, u32[]{:S(2)}, u32[]{:S(2)}) collective-permute-start(bf16[64,512]{0,1:T(8,128)(2,1)} %get-tuple-element.696), channel_id=1, source_target_pairs={{0,2},{1,3},{4,6},{5,7},{8,10},{9,11},{12,14},{13,15},{16,18},{17,... | collective-permute-start | bytes 196616 | tf_op jit(solution)/shard_map/while/body/eval_jaxpr/ppermute | solution.py:19
  133.2 3.8 %collective-permute-start.1 = (bf16[64,512]{0,1:T(8,128)(2,1)}, bf16[64,512]{0,1:T(8,128)(2,1)S(1)}, u32[]{:S(2)}, u32[]{:S(2)}) collective-permute-start(bf16[64,512]{0,1:T(8,128)(2,1)} %get-tuple-element.696), channel_id=1, source_target_pairs={{0,1},{1,2},{2,3},{4,5},{5,6},{6,7},{8,9},{9,10},{10,11},{12,13},{... | collective-permute-start | bytes 196616 | tf_op jit(solution)/shard_map/while/body/eval_jaxpr/ppermute | solution.py:19
  137.0 9.2 %collective-permute-start.2 = (bf16[64,1440]{1,0:T(8,128)(2,1)S(1)}, bf16[64,1440]{1,0:T(8,128)(2,1)S(1)}, u32[]{:S(2)}, u32[]{:S(2)}) collective-permute-start(bf16[64,1440]{1,0:T(8,128)(2,1)S(1)} %get-tuple-element.771), channel_id=1, source_target_pairs={{0,4},{4,8},{8,12},{1,5},{5,9},{9,13},{2,6},{6,10},{10,14},{3,7},{... | collective-permute-start | bytes 552968 | tf_op jit(solution)/shard_map/while/body/eval_jaxpr/ppermute | solution.py:19
  151.0 6.8 %collective-permute-start = (bf16[64,512]{0,1:T(8,128)(2,1)}, bf16[64,512]{0,1:T(8,128)(2,1)S(1)}, u32[]{:S(2)}, u32[]{:S(2)}) collective-permute-start(bf16[64,512]{0,1:T(8,128)(2,1)} %get-tuple-element.696), channel_id=1, source_target_pairs={{0,2},{1,3},{4,6},{5,7},{8,10},{9,11},{12,14},{13,15},{16,18},{17,... | collective-permute-start | bytes 196616 | tf_op jit(solution)/shard_map/while/body/eval_jaxpr/ppermute | solution.py:19
  154.0 3.8 %collective-permute-start.1 = (bf16[64,512]{0,1:T(8,128)(2,1)}, bf16[64,512]{0,1:T(8,128)(2,1)S(1)}, u32[]{:S(2)}, u32[]{:S(2)}) collective-permute-start(bf16[64,512]{0,1:T(8,128)(2,1)} %get-tuple-element.696), channel_id=1, source_target_pairs={{0,1},{1,2},{2,3},{4,5},{5,6},{6,7},{8,9},{9,10},{10,11},{12,13},{... | collective-permute-start | bytes 196616 | tf_op jit(solution)/shard_map/while/body/eval_jaxpr/ppermute | solution.py:19
  157.8 52.5 %collective-permute-start.2 = (bf16[64,1440]{1,0:T(8,128)(2,1)S(1)}, bf16[64,1440]{1,0:T(8,128)(2,1)S(1)}, u32[]{:S(2)}, u32[]{:S(2)}) collective-permute-start(bf16[64,1440]{1,0:T(8,128)(2,1)S(1)} %get-tuple-element.771), channel_id=1, source_target_pairs={{0,4},{4,8},{8,12},{1,5},{5,9},{9,13},{2,6},{6,10},{10,14},{3,7},{... | collective-permute-start | bytes 552968 | tf_op jit(solution)/shard_map/while/body/eval_jaxpr/ppermute | solution.py:19
  223.0 6.9 %collective-permute-start = (bf16[64,512]{0,1:T(8,128)(2,1)}, bf16[64,512]{0,1:T(8,128)(2,1)S(1)}, u32[]{:S(2)}, u32[]{:S(2)}) collective-permute-start(bf16[64,512]{0,1:T(8,128)(2,1)} %get-tuple-element.696), channel_id=1, source_target_pairs={{0,2},{1,3},{4,6},{5,7},{8,10},{9,11},{12,14},{13,15},{16,18},{17,... | collective-permute-start | bytes 196616 | tf_op jit(solution)/shard_map/while/body/eval_jaxpr/ppermute | solution.py:19
  225.4 4.6 %collective-permute-start.1 = (bf16[64,512]{0,1:T(8,128)(2,1)}, bf16[64,512]{0,1:T(8,128)(2,1)S(1)}, u32[]{:S(2)}, u32[]{:S(2)}) collective-permute-start(bf16[64,512]{0,1:T(8,128)(2,1)} %get-tuple-element.696), channel_id=1, source_target_pairs={{0,1},{1,2},{2,3},{4,5},{5,6},{6,7},{8,9},{9,10},{10,11},{12,13},{... | collective-permute-start | bytes 196616 | tf_op jit(solution)/shard_map/while/body/eval_jaxpr/ppermute | solution.py:19
  233.7 2.2 slice-start
  234.5 2.2 slice-start.1
  238.0 9.1 %collective-permute-start.2 = (bf16[64,1440]{1,0:T(8,128)(2,1)S(1)}, bf16[64,1440]{1,0:T(8,128)(2,1)S(1)}, u32[]{:S(2)}, u32[]{:S(2)}) collective-permute-start(bf16[64,1440]{1,0:T(8,128)(2,1)S(1)} %get-tuple-element.771), channel_id=1, source_target_pairs={{0,4},{4,8},{8,12},{1,5},{5,9},{9,13},{2,6},{6,10},{10,14},{3,7},{... | collective-permute-start | bytes 552968 | tf_op jit(solution)/shard_map/while/body/eval_jaxpr/ppermute | solution.py:19
  259.8 6.9 %collective-permute-start = (bf16[64,512]{0,1:T(8,128)(2,1)}, bf16[64,512]{0,1:T(8,128)(2,1)S(1)}, u32[]{:S(2)}, u32[]{:S(2)}) collective-permute-start(bf16[64,512]{0,1:T(8,128)(2,1)} %get-tuple-element.696), channel_id=1, source_target_pairs={{0,2},{1,3},{4,6},{5,7},{8,10},{9,11},{12,14},{13,15},{16,18},{17,... | collective-permute-start | bytes 196616 | tf_op jit(solution)/shard_map/while/body/eval_jaxpr/ppermute | solution.py:19
  262.1 4.6 %collective-permute-start.1 = (bf16[64,512]{0,1:T(8,128)(2,1)}, bf16[64,512]{0,1:T(8,128)(2,1)S(1)}, u32[]{:S(2)}, u32[]{:S(2)}) collective-permute-start(bf16[64,512]{0,1:T(8,128)(2,1)} %get-tuple-element.696), channel_id=1, source_target_pairs={{0,1},{1,2},{2,3},{4,5},{5,6},{6,7},{8,9},{9,10},{10,11},{12,13},{... | collective-permute-start | bytes 196616 | tf_op jit(solution)/shard_map/while/body/eval_jaxpr/ppermute | solution.py:19
  270.4 2.2 slice-start
  271.3 2.2 slice-start.1
  274.7 9.1 %collective-permute-start.2 = (bf16[64,1440]{1,0:T(8,128)(2,1)S(1)}, bf16[64,1440]{1,0:T(8,128)(2,1)S(1)}, u32[]{:S(2)}, u32[]{:S(2)}) collective-permute-start(bf16[64,1440]{1,0:T(8,128)(2,1)S(1)} %get-tuple-element.771), channel_id=1, source_target_pairs={{0,4},{4,8},{8,12},{1,5},{5,9},{9,13},{2,6},{6,10},{10,14},{3,7},{... | collective-permute-start | bytes 552968 | tf_op jit(solution)/shard_map/while/body/eval_jaxpr/ppermute | solution.py:19
  296.5 6.9 %collective-permute-start = (bf16[64,512]{0,1:T(8,128)(2,1)}, bf16[64,512]{0,1:T(8,128)(2,1)S(1)}, u32[]{:S(2)}, u32[]{:S(2)}) collective-permute-start(bf16[64,512]{0,1:T(8,128)(2,1)} %get-tuple-element.696), channel_id=1, source_target_pairs={{0,2},{1,3},{4,6},{5,7},{8,10},{9,11},{12,14},{13,15},{16,18},{17,... | collective-permute-start | bytes 196616 | tf_op jit(solution)/shard_map/while/body/eval_jaxpr/ppermute | solution.py:19
  298.9 4.6 %collective-permute-start.1 = (bf16[64,512]{0,1:T(8,128)(2,1)}, bf16[64,512]{0,1:T(8,128)(2,1)S(1)}, u32[]{:S(2)}, u32[]{:S(2)}) collective-permute-start(bf16[64,512]{0,1:T(8,128)(2,1)} %get-tuple-element.696), channel_id=1, source_target_pairs={{0,1},{1,2},{2,3},{4,5},{5,6},{6,7},{8,9},{9,10},{10,11},{12,13},{... | collective-permute-start | bytes 196616 | tf_op jit(solution)/shard_map/while/body/eval_jaxpr/ppermute | solution.py:19
  307.1 2.2 slice-start
  308.0 2.2 slice-start.1
  311.5 9.1 %collective-permute-start.2 = (bf16[64,1440]{1,0:T(8,128)(2,1)S(1)}, bf16[64,1440]{1,0:T(8,128)(2,1)S(1)}, u32[]{:S(2)}, u32[]{:S(2)}) collective-permute-start(bf16[64,1440]{1,0:T(8,128)(2,1)S(1)} %get-tuple-element.771), channel_id=1, source_target_pairs={{0,4},{4,8},{8,12},{1,5},{5,9},{9,13},{2,6},{6,10},{10,14},{3,7},{... | collective-permute-start | bytes 552968 | tf_op jit(solution)/shard_map/while/body/eval_jaxpr/ppermute | solution.py:19
  333.3 6.9 %collective-permute-start = (bf16[64,512]{0,1:T(8,128)(2,1)}, bf16[64,512]{0,1:T(8,128)(2,1)S(1)}, u32[]{:S(2)}, u32[]{:S(2)}) collective-permute-start(bf16[64,512]{0,1:T(8,128)(2,1)} %get-tuple-element.696), channel_id=1, source_target_pairs={{0,2},{1,3},{4,6},{5,7},{8,10},{9,11},{12,14},{13,15},{16,18},{17,... | collective-permute-start | bytes 196616 | tf_op jit(solution)/shard_map/while/body/eval_jaxpr/ppermute | solution.py:19
  335.6 4.6 %collective-permute-start.1 = (bf16[64,512]{0,1:T(8,128)(2,1)}, bf16[64,512]{0,1:T(8,128)(2,1)S(1)}, u32[]{:S(2)}, u32[]{:S(2)}) collective-permute-start(bf16[64,512]{0,1:T(8,128)(2,1)} %get-tuple-element.696), channel_id=1, source_target_pairs={{0,1},{1,2},{2,3},{4,5},{5,6},{6,7},{8,9},{9,10},{10,11},{12,13},{... | collective-permute-start | bytes 196616 | tf_op jit(solution)/shard_map/while/body/eval_jaxpr/ppermute | solution.py:19
  343.9 2.2 slice-start
  344.8 2.2 slice-start.1
  348.2 8.8 %collective-permute-start.2 = (bf16[64,1440]{1,0:T(8,128)(2,1)S(1)}, bf16[64,1440]{1,0:T(8,128)(2,1)S(1)}, u32[]{:S(2)}, u32[]{:S(2)}) collective-permute-start(bf16[64,1440]{1,0:T(8,128)(2,1)S(1)} %get-tuple-element.771), channel_id=1, source_target_pairs={{0,4},{4,8},{8,12},{1,5},{5,9},{9,13},{2,6},{6,10},{10,14},{3,7},{... | collective-permute-start | bytes 552968 | tf_op jit(solution)/shard_map/while/body/eval_jaxpr/ppermute | solution.py:19
Sparse Core Ops, SparseCore 0:
  9.5 45.0 all-gather.2
  56.2 46.3 all-gather.4
where the time goes:
time: 366 us; the launch traced here: 364 us
  waiting for transfers between devices  185 us (51%)
  local copies, waits for them, and re-layouts  49.8 us (14%)
  starting transfers between devices  36.5 us (10%)
  other arithmetic  35.7 us (10%)
  matrix products  28.7 us (8%)
  loops' own time  14.3 us (4%)
  between operations  14.1 us (4%)
    ppermute x21, waiting for transfers between devices, from_behind(): return lax.ppermute(block, axis, route)  92.9 us
    all_gather x1, waiting for transfers between devices, per_device(): lax.all_gather(w_out, 'seq', axis=1, tiled=True)  47.9 us
    all_gather x1, waiting for transfers between devices, per_device(): lax.all_gather(w_query, 'seq', axis=2, tiled=True)  43.2 us
    ppermute x21, starting transfers between devices, from_behind(): return lax.ppermute(block, axis, route)  36.5 us
    dot_general x4, matrix products, project(): jnp.dot(normed, query_weight, preferred_element_type=jnp.float32)  15.5 us
    another operation x1, loops' own time, per_device(): final = lax.fori_loop(0, micro + sections - 1, turn, initial)  13.4 us
    dynamic_update_slice x7, other arithmetic, turn(): lax.dynamic_update_index_in_dim(cache_buffer, jnp.where(active, cache, pr...  7.9 us
    another operation x13, local copies, waits for them, and re-layouts  7.83 us
  transfers between devices with their start and end apart: 23, of which 9 were waited for; matrix products, arithmetic and copies ran while one was open for 8% of the time, Pallas kernels for 0%

commit v1 on v0

v1 whole, which is shorter than its diff:
```python
import functools
import math

import jax
import jax.numpy as jnp
from jax import lax
from jax.experimental import pallas as pl
from jax.experimental.pallas import tpu as pltpu
from jax.sharding import PartitionSpec as P

HEAD_DIM = 64
WIN = 128
LANES = 128


THETA = 150000.0
EPSILON = 1e-05
MESH = pl.DeviceIdType.MESH
F32 = jnp.float32
BF16 = jnp.bfloat16
QUERY_CUTS = 3
OUT_CUTS = 4


def rotary(positions, head_size):
    half = head_size // 2
    freq = jnp.exp(jnp.arange(half, dtype=F32) * (-2.0 * math.log(THETA) / head_size))
    angles = positions.astype(F32)[:, None] * freq[None, :]
    return jnp.cos(angles), jnp.sin(angles)


def kernel(
    shape,
    order_ref, length_ref, sink_ref,
    tokens_ref, gain_ref, cos_ref, sin_ref, pair_ref, query_hbm, out_hbm,
    hidden_ref, cache_ref,
    query_w, out_w, arrive, window, hbuf, normed_ref, qbuf, cbuf,
    local_sem, x_send, x_recv, y_send, y_recv, d_send, d_recv, own_send, own_recv,
    w_send, w_recv, z_send, z_recv,
):
    groups, sections, seq = shape
    chips = seq // 2
    g = lax.axis_index("groups")
    sec = lax.axis_index("section")
    q = lax.axis_index("seq")
    chip, core = q // 2, q % 2
    partner = chip * 2 + (1 - core)
    micro, rows, width = tokens_ref.shape
    shard = query_w.shape[2]
    heads_width = seq * shard
    kv_width = pair_ref.shape[1] // 2
    kv_heads = kv_width // HEAD_DIM
    group = heads_width // kv_width
    keep = min(WIN, rows)
    depth = WIN // keep

    mine = [
        pltpu.make_async_copy(query_hbm, query_w.at[q], local_sem.at[0]),
        pltpu.make_async_copy(
            out_hbm, out_w.at[pl.ds(pl.multiple_of(q * shard, shard), shard)], local_sem.at[1]
        ),
    ]
    for copy in mine:
        copy.start()

    barrier = pltpu.get_barrier_semaphore()
    greeted = 0
    for d in range(1, seq):
        pl.semaphore_signal(barrier, 1, device_id={"seq": (q + d) % seq}, device_id_type=MESH)
        greeted += 1
    for e in range(1, groups):
        pl.semaphore_signal(barrier, 1, device_id={"groups": (g + e) % groups}, device_id_type=MESH)
        greeted += 1
    for s in sorted({1 % sections, (sections - 1) % sections} - {0}):
        pl.semaphore_signal(barrier, 1, device_id={"section": (sec + s) % sections}, device_id_type=MESH)
        greeted += 1
    for off in range(1, depth + 1):

        @pl.when(q < off)
        def _():
            window[:, off - 1] = jnp.zeros((micro, keep, 2 * kv_width), BF16)

    pl.semaphore_wait(barrier, greeted)

    cuts = (QUERY_CUTS, OUT_CUTS)
    lengths = (width // groups // QUERY_CUTS, shard // groups // OUT_CUTS)

    def piece(kind, owner, part, k):
        size = lengths[kind]
        first = (part * cuts[kind] + k) * size
        if kind == 0:
            return query_w.at[owner, pl.ds(pl.multiple_of(first, 16), size)]
        return out_w.at[pl.ds(pl.multiple_of(owner * shard + first, 16), size)]

    def whole(kind, owner):
        if kind == 0:
            return query_w.at[owner]
        return out_w.at[pl.ds(pl.multiple_of(owner * shard, shard), shard)]

    def remote(ref, send, recv, target):
        return pltpu.make_async_remote_copy(
            src_ref=ref, dst_ref=ref, send_sem=send, recv_sem=recv,
            device_id=target, device_id_type=MESH,
        )

    def x_copy(kind, d, k, owner):
        return remote(
            piece(kind, owner, g, k), x_send.at[kind, d, k], x_recv.at[kind, d, k],
            {"seq": ((chip + d) % chips) * 2 + core},
        )

    def y_copy(kind, d, k, e, owner, part):
        return remote(
            piece(kind, owner, part, k), y_send.at[kind, d, k, e], y_recv.at[kind, d, k, e],
            {"groups": (g + e) % groups},
        )

    def d_copy(kind, d, k, e, owner):
        return remote(
            piece(kind, owner, (g - e + groups) % groups, k), d_send.at[kind, d, k, e],
            d_recv.at[kind, d, k, e], {"seq": partner},
        )

    def own_copy(kind, owner):
        return remote(whole(kind, owner), own_send.at[kind], own_recv.at[kind], {"seq": partner})

    plan = [(kind, k, d) for kind in range(2) for k in range(cuts[kind]) for d in range(1, chips)]
    for kind in range(2):
        mine[kind].wait()
        for k in range(cuts[kind]):
            for d in range(1, chips):
                x_copy(kind, d, k, q).start()
        own_copy(kind, q).start()

    def source(d, which):
        return ((chip - d + chips) % chips) * 2 + which

    def relay_y(kind, k, d):
        for e in range(1, groups):
            y_copy(kind, d, k, e, source(d, core), (g - e + groups) % groups).wait_recv()
            d_copy(kind, d, k, e, source(d, core)).start()

    previous = None
    for kind, k, d in plan:
        x_copy(kind, d, k, source(d, core)).wait_recv()
        for e in range(1, groups):
            y_copy(kind, d, k, e, source(d, core), g).start()
        d_copy(kind, d, k, 0, source(d, core)).start()
        if previous is not None:
            relay_y(*previous)
        previous = (kind, k, d)
    if previous is not None:
        relay_y(*previous)
    for kind in range(2):
        own_copy(kind, partner).wait_recv()
    for kind, k, d in plan:
        for e in range(groups):
            d_copy(kind, d, k, e, source(d, 1 - core)).wait_recv()

    lane = lax.broadcasted_iota(jnp.int32, (rows, LANES), 1)
    first_half = (lane % HEAD_DIM) < (HEAD_DIM // 2)
    low = lane < HEAD_DIM
    cosine = cos_ref[...]
    sine = sin_ref[...]
    half = HEAD_DIM // 2

    def rotate(tile):
        swapped = jnp.where(
            first_half, pltpu.roll(tile, LANES - half, 1), pltpu.roll(tile, half, 1)
        )
        return tile * cosine + swapped * sine

    def z_copy(t):
        return pltpu.make_async_remote_copy(
            src_ref=hidden_ref.at[t], dst_ref=arrive.at[t], send_sem=z_send.at[t],
            recv_sem=z_recv.at[t], device_id={"section": (sec + 1) % sections}, device_id_type=MESH,
        )

    def w_copy(t, off):
        return pltpu.make_async_remote_copy(
            src_ref=cache_ref.at[t, pl.ds(rows - keep, keep)], dst_ref=window.at[t, off - 1],
            send_sem=w_send.at[t, off - 1], recv_sem=w_recv.at[t, off - 1],
            device_id={"seq": (q + off) % seq}, device_id_type=MESH,
        )

    def slot(t, carry):
        block = order_ref[t]
        length = length_ref[block]

        @pl.when(sec == 0)
        def _():
            hbuf[...] = tokens_ref[block]

        @pl.when(sec > 0)
        def _():
            z_copy(t).wait_recv()
            hbuf[...] = arrive[t]

        widened = hbuf[...].astype(F32)
        scale = lax.rsqrt(jnp.mean(widened * widened, -1, keepdims=True) + EPSILON)
        normed_ref[...] = (widened * scale * gain_ref[...]).astype(BF16)
        normed = normed_ref[...]
        projected = jnp.dot(normed, pair_ref[...], preferred_element_type=F32)
        for p in range(kv_width // LANES):
            tile = slice(p * LANES, (p + 1) * LANES)
            cache_ref[t, :, tile] = rotate(projected[:, tile]).astype(BF16)
        cache_ref[t, :, kv_width:] = projected[:, kv_width:].astype(BF16)
        for off in range(1, depth + 1):

            @pl.when(q + off < seq)
            def _():
                w_copy(t, off).start()

        for s in range(seq):
            queries = jnp.dot(normed, query_w[s], preferred_element_type=F32)
            for p in range(shard // LANES):
                rotated = rotate(queries[:, p * LANES:(p + 1) * LANES]) * 0.125
                qbuf[:, s * shard + p * LANES:s * shard + (p + 1) * LANES] = rotated.astype(BF16)

        for off in range(1, depth + 1):

            @pl.when(q >= off)
            def _():
                w_copy(t, off).wait_recv()

        span = WIN + rows
        row = lax.broadcasted_iota(jnp.int32, (rows, span), 0)
        col = lax.broadcasted_iota(jnp.int32, (rows, span), 1) - WIN
        column = col + q * rows
        allowed = (col <= row) & (row - col < WIN) & (column >= 0)
        allowed = allowed & ((column < length) | (col == row))
        bias = jnp.where(allowed, F32(0.0), F32(-1e30))
        tiles = group // 2
        for h in range(kv_heads):
            def span_of(first):
                at = slice(first, first + HEAD_DIM)
                parts = [window[t, off - 1, :, at] for off in range(depth, 0, -1)]
                head = jnp.concatenate(parts + [cache_ref[t, :, at]], 0)
                return jnp.concatenate([head, head], 1)

            keys = span_of(h * HEAD_DIM)
            values = span_of(kv_width + h * HEAD_DIM)
            stack, sinks = [], []
            for p in range(tiles):
                at = (h * tiles + p) * LANES
                pair = qbuf[:, at:at + LANES]
                zero = jnp.zeros_like(pair)
                stack += [jnp.where(low, pair, zero), jnp.where(low, zero, pair)]
                for j in range(2):
                    sinks.append(jnp.full((1, rows, 1), sink_ref[h * group + 2 * p + j], F32))
            sink = jnp.concatenate(sinks, 0)
            scores = lax.dot_general(
                jnp.concatenate(stack, 0), keys, (((1,), (1,)), ((), ())),
                preferred_element_type=F32,
            ).reshape(group, rows, span)
            masked = jnp.where(bias[None] < 0, F32(-1e30), scores)
            top = jnp.maximum(jnp.max(masked, -1, keepdims=True), sink)
            expo = jnp.exp(masked - top)
            total = jnp.sum(expo, -1, keepdims=True) + jnp.exp(sink - top)
            weights = (expo * (1.0 / total)).astype(BF16).reshape(group * rows, span)
            context = jnp.dot(weights, values, preferred_element_type=F32)
            for p in range(tiles):
                at = (h * tiles + p) * LANES
                one = context[2 * p * rows:(2 * p + 1) * rows]
                two = context[(2 * p + 1) * rows:(2 * p + 2) * rows]
                cbuf[:, at:at + LANES] = jnp.where(low, one, two).astype(BF16)
        output = jnp.dot(cbuf[...], out_w[...], preferred_element_type=F32)
        hidden_ref[t] = (hbuf[...].astype(F32) + output).astype(BF16)

        @pl.when(sec + 1 < sections)
        def _():
            z_copy(t).start()

        return carry

    lax.fori_loop(0, micro, slot, 0)

    for kind, k, d in plan:
        x_copy(kind, d, k, q).wait_send()
        for e in range(1, groups):
            y_copy(kind, d, k, e, source(d, core), g).wait_send()
        for e in range(groups):
            d_copy(kind, d, k, e, source(d, core)).wait_send()
    for kind in range(2):
        own_copy(kind, q).wait_send()
    for t in range(micro):
        for off in range(1, depth + 1):

            @pl.when(q + off < seq)
            def _():
                w_copy(t, off).wait_send()

        @pl.when(sec + 1 < sections)
        def _():
            z_copy(t).wait_send()


def per_device(
    shape,
    tokens, block_order, prompt_lengths, norm_gain, w_query, w_key_value, w_out, sink_logits
):
    groups, sections, seq = shape
    micro, rows, width = tokens.shape
    shard = w_query.shape[2]
    pair_width = w_key_value.shape[2]
    chips = seq // 2
    keep = min(WIN, rows)
    depth = WIN // keep
    positions = lax.axis_index("seq") * rows + jnp.arange(rows, dtype=jnp.int32)
    cosine, sine = rotary(positions, HEAD_DIM)
    repeat = LANES // HEAD_DIM
    cosine = jnp.tile(jnp.concatenate([cosine, cosine], 1), (1, repeat))
    sine = jnp.tile(jnp.concatenate([-sine, sine], 1), (1, repeat))
    most = max(QUERY_CUTS, OUT_CUTS)
    dma = pltpu.SemaphoreType.DMA
    vmem = pl.BlockSpec(memory_space=pltpu.VMEM)
    smem = pl.BlockSpec(memory_space=pltpu.SMEM)
    hbm = pl.BlockSpec(memory_space=pl.ANY)
    hidden, cache = pl.pallas_call(
        functools.partial(kernel, shape),
        out_shape=(
            jax.ShapeDtypeStruct((micro, rows, width), BF16),
            jax.ShapeDtypeStruct((micro, rows, pair_width), BF16),
        ),
        in_specs=[smem] * 3 + [vmem] * 5 + [hbm] * 2,
        out_specs=(vmem, vmem),
        scratch_shapes=[
            pltpu.VMEM((seq, width, shard), BF16),
            pltpu.VMEM((seq * shard, width), BF16),
            pltpu.VMEM((micro, rows, width), BF16),
            pltpu.VMEM((micro, depth, keep, pair_width), BF16),
            pltpu.VMEM((rows, width), BF16),
            pltpu.VMEM((rows, width), BF16),
            pltpu.VMEM((rows, seq * shard), BF16),
            pltpu.VMEM((rows, seq * shard), BF16),
            dma((2,)),
            dma((2, chips, most)),
            dma((2, chips, most)),
            dma((2, chips, most, groups)),
            dma((2, chips, most, groups)),
            dma((2, chips, most, groups)),
            dma((2, chips, most, groups)),
            dma((2,)),
            dma((2,)),
            dma((micro, depth)),
            dma((micro, depth)),
            dma((micro,)),
            dma((micro,)),
        ],
        compiler_params=pltpu.CompilerParams(
            collective_id=0, has_side_effects=True, vmem_limit_bytes=50 * 1024 * 1024
        ),
    )(
        block_order, prompt_lengths, sink_logits[0],
        tokens, norm_gain, cosine, sine, w_key_value[0], w_query[0], w_out[0],
    )
    return hidden[None], cache[None]


def solution(mesh):
    in_specs = (
        P("groups", "seq", None),
        P("groups"),
        P("groups"),
        P("section", None),
        P("section", None, "seq"),
        P("section", None, None),
        P("section", "seq", None),
        P("section", None),
    )
    out_specs = (P("section", "groups", "seq", None), P("section", "groups", "seq", None))
    shape = tuple(mesh.shape[name] for name in ("groups", "section", "seq"))
    return jax.shard_map(
        functools.partial(per_device, shape),
        mesh=mesh, in_specs=in_specs, out_specs=out_specs, check_vma=False,
    )
```

time: 366 us -> 125 us (0.34)
  the two profiles are of different devices: /device:TPU:28 before, /device:TPU:27 now
where the time goes in v1:
time: 125 us
  Pallas kernels  120 us (96%)
  local copies, waits for them, and re-layouts  4.6 us (4%)
    pallas_call x1, Pallas kernels, per_device(): pl.pallas_call(functools.partial(kernel, shape), out_shape=(jax.ShapeDtyp...  120 us
    unnamed x15, local copies, waits for them, and re-layouts  4.35 us

profile of v1, /device:TPU:27, one launch (start us, length us, event | category | flops | bytes accessed | tf_op | source)
XLA Modules:
  0.0 125.3 jit_solution(5524854373633540106)
XLA Ops:
  0.7 0.2 fusion
  0.9 0.1 pad_maximum_fusion
  1.0 0.1 tile.9.cos_ref
  1.1 0.1 tile.21.sin_ref
  1.2 0.0 copy-start
  1.2 0.0 copy-start.1
  1.2 0.0 copy-start.2
  1.2 0.0 copy-start.3
  1.2 0.0 copy-start.4
  1.3 0.0 copy-start.5
  1.3 2.7 %copy.10 = bf16[1,512,1440]{2,1,0:T(8,128)(2,1)} copy(bf16[1,512,1440]{1,2,0:T(8,128)(2,1)} %param.14) | data formatting | bytes 2949120 | tf_op args[6]
  4.0 0.0 copy-done
  4.0 0.0 copy-done.1
  4.0 0.0 copy-done.2
  4.0 0.0 copy-done.3
  4.0 0.0 copy-done.4
  4.0 0.0 copy-done.5
  4.0 119.7 %shard_map.95 = (bf16[4,64,1440]{2,1,0:T(8,128)(2,1)S(1)}, bf16[4,64,512]{2,1,0:T(8,128)(2,1)S(1)}) custom-call(s32[4]{0:T(128)S(1)} %copy-done.3, s32[4]{0:T(128)S(1)} %copy-done.4, f32[32]{0:T(128)S(1)} %bitcast.9, bf16[4,64,1440]{2,1,0:T(8,128)(2,1)S(1)} %copy-done.1, f32[1,1440]{1,0:T(1,128)S(1)} %copy-done.2, f32[64,128]{1,0:T(8,128)S(1)} %tile.9.cos_ref, ...), custom_call_target="tpu_custom_call" | custom-call | tf_op jit(solution)/shard_map/pallas_call | solution.py:319
  123.7 0.9 copy.13
  124.6 0.7 copy.14
  (4 shorter events, 0.1 us)
Async XLA Ops:
  1.2 2.8 %copy-start = (bf16[1,1440,512]{2,1,0:T(8,128)(2,1)S(1)}, bf16[1,1440,512]{2,1,0:T(8,128)(2,1)}, u32[]{:S(2)}) copy-start(bf16[1,1440,512]{2,1,0:T(8,128)(2,1)} %param.13) | copy-start | bytes 4423684
  1.2 2.8 %copy-start.1 = (bf16[4,64,1440]{2,1,0:T(8,128)(2,1)S(1)}, bf16[4,64,1440]{2,1,0:T(8,128)(2,1)}, u32[]{:S(2)}) copy-start(bf16[4,64,1440]{2,1,0:T(8,128)(2,1)} %tokens_ref.1) | copy-start | bytes 2211844
  1.2 2.8 %copy-start.2 = (f32[1,1440]{1,0:T(1,128)S(1)}, f32[1,1440]{1,0:T(1,128)}, u32[]{:S(2)}) copy-start(f32[1,1440]{1,0:T(1,128)} %gain_ref.1) | copy-start | bytes 17284
  1.2 2.8 %copy-start.3 = (s32[4]{0:T(128)S(1)}, s32[4]{0:T(128)}, u32[]{:S(2)}) copy-start(s32[4]{0:T(128)} %order_ref.1) | copy-start | bytes 52
  1.2 2.8 %copy-start.4 = (s32[4]{0:T(128)S(1)}, s32[4]{0:T(128)}, u32[]{:S(2)}) copy-start(s32[4]{0:T(128)} %length_ref.1) | copy-start | bytes 52
  1.3 2.8 %copy-start.5 = (f32[1,32]{1,0:T(1,128)S(1)}, f32[1,32]{1,0:T(1,128)}, u32[]{:S(2)}) copy-start(f32[1,32]{1,0:T(1,128)} %param.15) | copy-start | bytes 388

commit v2 on v1

--- a/solution.py
+++ b/solution.py
@@ -19,7 +19,9 @@
 F32 = jnp.float32
 BF16 = jnp.bfloat16
 QUERY_CUTS = 3
-OUT_CUTS = 4
+OUT_CUTS = 3
+HOP_CUTS = 3
+EARLY = 4
 
 
 def rotary(positions, head_size):
@@ -57,7 +59,7 @@
     mine = [
         pltpu.make_async_copy(query_hbm, query_w.at[q], local_sem.at[0]),
         pltpu.make_async_copy(
-            out_hbm, out_w.at[pl.ds(pl.multiple_of(q * shard, shard), shard)], local_sem.at[1]
+            out_hbm, out_w.at[:, pl.ds(pl.multiple_of(q * shard, shard), shard)], local_sem.at[1]
         ),
     ]
     for copy in mine:
@@ -83,19 +85,21 @@
     pl.semaphore_wait(barrier, greeted)
 
     cuts = (QUERY_CUTS, OUT_CUTS)
-    lengths = (width // groups // QUERY_CUTS, shard // groups // OUT_CUTS)
+    lengths = (width // groups // QUERY_CUTS, width // groups // OUT_CUTS)
 
     def piece(kind, owner, part, k):
         size = lengths[kind]
         first = (part * cuts[kind] + k) * size
         if kind == 0:
             return query_w.at[owner, pl.ds(pl.multiple_of(first, 16), size)]
-        return out_w.at[pl.ds(pl.multiple_of(owner * shard + first, 16), size)]
+        return out_w.at[
+            pl.ds(pl.multiple_of(first, 16), size), pl.ds(pl.multiple_of(owner * shard, shard), shard)
+        ]
 
     def whole(kind, owner):
         if kind == 0:
             return query_w.at[owner]
-        return out_w.at[pl.ds(pl.multiple_of(owner * shard, shard), shard)]
+        return out_w.at[:, pl.ds(pl.multiple_of(owner * shard, shard), shard)]
 
     def remote(ref, send, recv, target):
         return pltpu.make_async_remote_copy(
@@ -131,6 +135,78 @@
             for d in range(1, chips):
                 x_copy(kind, d, k, q).start()
         own_copy(kind, q).start()
+
+    lane = lax.broadcasted_iota(jnp.int32, (rows, LANES), 1)
+    first_half = (lane % HEAD_DIM) < (HEAD_DIM // 2)
+    low = lane < HEAD_DIM
+    cosine = cos_ref[...]
+    sine = sin_ref[...]
+    half = HEAD_DIM // 2
+
+    def rotate(tile):
+        swapped = jnp.where(
+            first_half, pltpu.roll(tile, LANES - half, 1), pltpu.roll(tile, half, 1)
+        )
+        return tile * cosine + swapped * sine
+
+    step = -(-width // (HOP_CUTS * LANES)) * LANES
+    edges = [(c * step, min(step, width - c * step)) for c in range(HOP_CUTS)]
+
+    def z_copy(t, c):
+        columns = pl.ds(*edges[c])
+        return pltpu.make_async_remote_copy(
+            src_ref=hidden_ref.at[t, :, columns], dst_ref=arrive.at[t, :, columns],
+            send_sem=z_send.at[t, c], recv_sem=z_recv.at[t, c], device_id={"section": (sec + 1) % sections}, device_id_type=MESH,
+        )
+
+    def w_copy(t, off, side):
+        columns = pl.ds(side * kv_width, kv_width)
+        return pltpu.make_async_remote_copy(
+            src_ref=cache_ref.at[t, pl.ds(rows - keep, keep), columns],
+            dst_ref=window.at[t, off - 1, :, columns],
+            send_sem=w_send.at[t, off - 1, side], recv_sem=w_recv.at[t, off - 1, side],
+            device_id={"seq": (q + off) % seq}, device_id_type=MESH,
+        )
+
+    def enter(t):
+        block = order_ref[t]
+
+        @pl.when(sec == 0)
+        def _():
+            hbuf[t] = tokens_ref[block]
+
+        @pl.when(sec > 0)
+        def _():
+            for c in range(HOP_CUTS):
+                z_copy(t, c).wait_recv()
+            hbuf[t] = arrive[t]
+
+        widened = hbuf[t].astype(F32)
+        scale = lax.rsqrt(jnp.mean(widened * widened, -1, keepdims=True) + EPSILON)
+        normed_ref[t] = (widened * scale * gain_ref[...]).astype(BF16)
+        keys = jnp.dot(normed_ref[t], pair_ref[:, :kv_width], preferred_element_type=F32)
+        for p in range(kv_width // LANES):
+            tile = slice(p * LANES, (p + 1) * LANES)
+            cache_ref[t, :, tile] = rotate(keys[:, tile]).astype(BF16)
+        for off in range(1, depth + 1):
+
+            @pl.when(q + off < seq)
+            def _():
+                w_copy(t, off, 0).start()
+
+        values = jnp.dot(normed_ref[t], pair_ref[:, kv_width:], preferred_element_type=F32)
+        cache_ref[t, :, kv_width:] = values.astype(BF16)
+        for off in range(1, depth + 1):
+
+            @pl.when(q + off < seq)
+            def _():
+                w_copy(t, off, 1).start()
+
+    @pl.when(sec == 0)
+    def _():
+        @pl.loop(0, micro)
+        def _(t):
+            enter(t)
 
     def source(d, which):
         return ((chip - d + chips) % chips) * 2 + which
@@ -157,71 +233,31 @@
         for e in range(groups):
             d_copy(kind, d, k, e, source(d, 1 - core)).wait_recv()
 
-    lane = lax.broadcasted_iota(jnp.int32, (rows, LANES), 1)
-    first_half = (lane % HEAD_DIM) < (HEAD_DIM // 2)
-    low = lane < HEAD_DIM
-    cosine = cos_ref[...]
-    sine = sin_ref[...]
-    half = HEAD_DIM // 2
-
-    def rotate(tile):
-        swapped = jnp.where(
-            first_half, pltpu.roll(tile, LANES - half, 1), pltpu.roll(tile, half, 1)
-        )
-        return tile * cosine + swapped * sine
-
-    def z_copy(t):
-        return pltpu.make_async_remote_copy(
-            src_ref=hidden_ref.at[t], dst_ref=arrive.at[t], send_sem=z_send.at[t],
-            recv_sem=z_recv.at[t], device_id={"section": (sec + 1) % sections}, device_id_type=MESH,
-        )
-
-    def w_copy(t, off):
-        return pltpu.make_async_remote_copy(
-            src_ref=cache_ref.at[t, pl.ds(rows - keep, keep)], dst_ref=window.at[t, off - 1],
-            send_sem=w_send.at[t, off - 1], recv_sem=w_recv.at[t, off - 1],
-            device_id={"seq": (q + off) % seq}, device_id_type=MESH,
-        )
-
     def slot(t, carry):
-        block = order_ref[t]
-        length = length_ref[block]
-
-        @pl.when(sec == 0)
-        def _():
-            hbuf[...] = tokens_ref[block]
-
         @pl.when(sec > 0)
         def _():
-            z_copy(t).wait_recv()
-            hbuf[...] = arrive[t]
-
-        widened = hbuf[...].astype(F32)
-        scale = lax.rsqrt(jnp.mean(widened * widened, -1, keepdims=True) + EPSILON)
-        normed_ref[...] = (widened * scale * gain_ref[...]).astype(BF16)
-        normed = normed_ref[...]
-        projected = jnp.dot(normed, pair_ref[...], preferred_element_type=F32)
-        for p in range(kv_width // LANES):
-            tile = slice(p * LANES, (p + 1) * LANES)
-            cache_ref[t, :, tile] = rotate(projected[:, tile]).astype(BF16)
-        cache_ref[t, :, kv_width:] = projected[:, kv_width:].astype(BF16)
-        for off in range(1, depth + 1):
-
-            @pl.when(q + off < seq)
-            def _():
-                w_copy(t, off).start()
-
-        for s in range(seq):
+            enter(t)
+
+        length = length_ref[order_ref[t]]
+        normed = normed_ref[t]
+
+        def ask(s):
             queries = jnp.dot(normed, query_w[s], preferred_element_type=F32)
             for p in range(shard // LANES):
                 rotated = rotate(queries[:, p * LANES:(p + 1) * LANES]) * 0.125
                 qbuf[:, s * shard + p * LANES:s * shard + (p + 1) * LANES] = rotated.astype(BF16)
 
+        per_head = seq // kv_heads
+        early = min(EARLY, kv_heads)
+        for s in range(early * per_head):
+            ask(s)
+
         for off in range(1, depth + 1):
 
             @pl.when(q >= off)
             def _():
-                w_copy(t, off).wait_recv()
+                w_copy(t, off, 0).wait_recv()
+                w_copy(t, off, 1).wait_recv()
 
         span = WIN + rows
         row = lax.broadcasted_iota(jnp.int32, (rows, span), 0)
@@ -231,45 +267,65 @@
         allowed = allowed & ((column < length) | (col == row))
         bias = jnp.where(allowed, F32(0.0), F32(-1e30))
         tiles = group // 2
-        for h in range(kv_heads):
-            def span_of(first):
-                at = slice(first, first + HEAD_DIM)
-                parts = [window[t, off - 1, :, at] for off in range(depth, 0, -1)]
-                head = jnp.concatenate(parts + [cache_ref[t, :, at]], 0)
-                return jnp.concatenate([head, head], 1)
-
-            keys = span_of(h * HEAD_DIM)
-            values = span_of(kv_width + h * HEAD_DIM)
-            stack, sinks = [], []
+
+        def span_of(first):
+            at = slice(first, first + HEAD_DIM)
+            parts = [window[t, off - 1, :, at] for off in range(depth, 0, -1)]
+            return jnp.concatenate(parts + [cache_ref[t, :, at]], 0)
+
+        def score(h):
+            head = span_of(h * HEAD_DIM)
+            stack = []
             for p in range(tiles):
                 at = (h * tiles + p) * LANES
                 pair = qbuf[:, at:at + LANES]
                 zero = jnp.zeros_like(pair)
                 stack += [jnp.where(low, pair, zero), jnp.where(low, zero, pair)]
-                for j in range(2):
-                    sinks.append(jnp.full((1, rows, 1), sink_ref[h * group + 2 * p + j], F32))
-            sink = jnp.concatenate(sinks, 0)
-            scores = lax.dot_general(
-                jnp.concatenate(stack, 0), keys, (((1,), (1,)), ((), ())),
-                preferred_element_type=F32,
-            ).reshape(group, rows, span)
-            masked = jnp.where(bias[None] < 0, F32(-1e30), scores)
-            top = jnp.maximum(jnp.max(masked, -1, keepdims=True), sink)
-            expo = jnp.exp(masked - top)
-            total = jnp.sum(expo, -1, keepdims=True) + jnp.exp(sink - top)
-            weights = (expo * (1.0 / total)).astype(BF16).reshape(group * rows, span)
-            context = jnp.dot(weights, values, preferred_element_type=F32)
+            return lax.dot_general(
+                jnp.concatenate(stack, 0), jnp.concatenate([head, head], 1),
+                (((1,), (1,)), ((), ())), preferred_element_type=F32,
+            )
+
+        def mix(h, scores):
+            head = span_of(kv_width + h * HEAD_DIM)
+            values = jnp.concatenate([head, head, jnp.ones((span, LANES), BF16)], 1)
+            expos, rest = [], []
+            for j in range(group):
+                sink = sink_ref[h * group + j]
+                masked = scores[j * rows:(j + 1) * rows] + bias
+                top = jnp.maximum(jnp.max(masked, -1, keepdims=True), sink)
+                expos.append(jnp.exp(masked - top).astype(BF16))
+                rest.append(jnp.exp(sink - top))
+            summed = jnp.dot(jnp.concatenate(expos, 0), values, preferred_element_type=F32)
             for p in range(tiles):
                 at = (h * tiles + p) * LANES
-                one = context[2 * p * rows:(2 * p + 1) * rows]
-                two = context[(2 * p + 1) * rows:(2 * p + 2) * rows]
-                cbuf[:, at:at + LANES] = jnp.where(low, one, two).astype(BF16)
-        output = jnp.dot(cbuf[...], out_w[...], preferred_element_type=F32)
-        hidden_ref[t] = (hbuf[...].astype(F32) + output).astype(BF16)
-
-        @pl.when(sec + 1 < sections)
-        def _():
-            z_copy(t).start()
+                sides = []
+                for j in (2 * p, 2 * p + 1):
+                    some = summed[j * rows:(j + 1) * rows]
+                    sides.append((some[:, :LANES], some[:, LANES:] + rest[j]))
+                context = jnp.where(low, sides[0][0], sides[1][0])
+                context = context / jnp.where(low, sides[0][1], sides[1][1])
+                cbuf[:, at:at + LANES] = context.astype(BF16)
+
+        scores = score(0)
+        for h in range(kv_heads):
+            following = score(h + 1) if h + 1 < kv_heads else None
+            if h + early < kv_heads:
+                for s in range((h + early) * per_head, (h + early + 1) * per_head):
+                    ask(s)
+            mix(h, scores)
+            scores = following
+        for c, (first, size) in enumerate(edges):
+            output = lax.dot_general(
+                cbuf[...], out_w[first:first + size], (((1,), (1,)), ((), ())),
+                preferred_element_type=F32,
+            )
+            columns = slice(first, first + size)
+            hidden_ref[t, :, columns] = (hbuf[t, :, columns].astype(F32) + output).astype(BF16)
+
+            @pl.when(sec + 1 < sections)
+            def _():
+                z_copy(t, c).start()
 
         return carry
 
@@ -288,11 +344,13 @@
 
             @pl.when(q + off < seq)
             def _():
-                w_copy(t, off).wait_send()
+                w_copy(t, off, 0).wait_send()
+                w_copy(t, off, 1).wait_send()
 
         @pl.when(sec + 1 < sections)
         def _():
-            z_copy(t).wait_send()
+            for c in range(HOP_CUTS):
+                z_copy(t, c).wait_send()
 
 
 def per_device(
@@ -326,11 +384,11 @@
         out_specs=(vmem, vmem),
         scratch_shapes=[
             pltpu.VMEM((seq, width, shard), BF16),
-            pltpu.VMEM((seq * shard, width), BF16),
+            pltpu.VMEM((width, seq * shard), BF16),
             pltpu.VMEM((micro, rows, width), BF16),
             pltpu.VMEM((micro, depth, keep, pair_width), BF16),
-            pltpu.VMEM((rows, width), BF16),
-            pltpu.VMEM((rows, width), BF16),
+            pltpu.VMEM((micro, rows, width), BF16),
+            pltpu.VMEM((micro, rows, width), BF16),
             pltpu.VMEM((rows, seq * shard), BF16),
             pltpu.VMEM((rows, seq * shard), BF16),
             dma((2,)),
@@ -342,17 +400,17 @@
             dma((2, chips, most, groups)),
             dma((2,)),
             dma((2,)),
-            dma((micro, depth)),
-            dma((micro, depth)),
-            dma((micro,)),
-            dma((micro,)),
+            dma((micro, depth, 2)),
+            dma((micro, depth, 2)),
+            dma((micro, HOP_CUTS)),
+            dma((micro, HOP_CUTS)),
         ],
         compiler_params=pltpu.CompilerParams(
             collective_id=0, has_side_effects=True, vmem_limit_bytes=50 * 1024 * 1024
         ),
     )(
         block_order, prompt_lengths, sink_logits[0],
-        tokens, norm_gain, cosine, sine, w_key_value[0], w_query[0], w_out[0],
+        tokens, norm_gain, cosine, sine, w_key_value[0], w_query[0], w_out[0].T,
     )
     return hidden[None], cache[None]
 

time: 125 us -> 106 us (0.85)
  Pallas kernels: 120 us -> 97.9 us
  local copies, waits for them, and re-layouts: 4.6 us -> 7 us
    pallas_call x1, Pallas kernels: 120 us -> 97.9 us  [per_device(): pl.pallas_call(functools.partial(kernel, shape), out_shape=(jax.ShapeDtyp...]
    unnamed x15 -> x14, local copies, waits for them, and re-layouts: 4.35 us -> 6.75 us
where the time goes in v2:
time: 106 us
  Pallas kernels  97.9 us (92%)
  local copies, waits for them, and re-layouts  7 us (7%)
    pallas_call x1, Pallas kernels, per_device(): pl.pallas_call(functools.partial(kernel, shape), out_shape=(jax.ShapeDtyp...  97.9 us
    unnamed x14, local copies, waits for them, and re-layouts  6.75 us

profile of v2, /device:TPU:27, one launch (start us, length us, event | category | flops | bytes accessed | tf_op | source)
XLA Modules:
  0.0 105.9 jit_solution(5499627123006556938)
XLA Ops:
  0.7 0.2 fusion
  0.9 0.1 pad_maximum_fusion
  1.0 0.1 tile.9.cos_ref
  1.1 0.1 tile.21.sin_ref
  1.2 0.0 copy-start
  1.2 1.4 %copy-done = bf16[1,1440,512]{2,1,0:T(8,128)(2,1)S(1)} copy-done((bf16[1,1440,512]{2,1,0:T(8,128)(2,1)S(1)}, bf16[1,1440,512]{2,1,0:T(8,128)(2,1)}, u32[]{:S(2)}) %copy-start) | copy-done | bytes 1474584
  2.6 0.0 copy-start.1
  2.6 1.1 %copy-done.1 = bf16[4,64,1440]{2,1,0:T(8,128)(2,1)S(1)} copy-done((bf16[4,64,1440]{2,1,0:T(8,128)(2,1)S(1)}, bf16[4,64,1440]{2,1,0:T(8,128)(2,1)}, u32[]{:S(2)}) %copy-start.1) | copy-done | bytes 737304
  3.7 0.0 copy-start.2
  3.7 0.7 copy-done.2
  4.4 0.0 copy-start.3
  4.4 0.7 copy-done.3
  5.1 0.0 copy-start.4
  5.1 0.7 copy-done.4
  5.7 0.0 copy-start.5
  5.7 0.7 copy-done.5
  6.4 97.9 %shard_map.95 = (bf16[4,64,1440]{2,1,0:T(8,128)(2,1)S(1)}, bf16[4,64,512]{2,1,0:T(8,128)(2,1)S(1)}) custom-call(s32[4]{0:T(128)S(1)} %copy-done.3, s32[4]{0:T(128)S(1)} %copy-done.4, f32[32]{0:T(128)S(1)} %bitcast.11, bf16[4,64,1440]{2,1,0:T(8,128)(2,1)S(1)} %copy-done.1, f32[1,1440]{1,0:T(1,128)S(1)} %copy-done.2, f32[64,128]{1,0:T(8,128)S(1)} %tile.9.cos_ref, ...), custom_call_target="tpu_custom_call" | custom-call | tf_op jit(solution)/shard_map/pallas_call | solution.py:377
  104.3 0.9 copy.12
  105.2 0.7 copy.13
  (4 shorter events, 0.1 us)
Async XLA Ops:
  1.2 1.4 %copy-start = (bf16[1,1440,512]{2,1,0:T(8,128)(2,1)S(1)}, bf16[1,1440,512]{2,1,0:T(8,128)(2,1)}, u32[]{:S(2)}) copy-start(bf16[1,1440,512]{2,1,0:T(8,128)(2,1)} %param.13) | copy-start | bytes 4423684
  2.6 1.1 %copy-start.1 = (bf16[4,64,1440]{2,1,0:T(8,128)(2,1)S(1)}, bf16[4,64,1440]{2,1,0:T(8,128)(2,1)}, u32[]{:S(2)}) copy-start(bf16[4,64,1440]{2,1,0:T(8,128)(2,1)} %tokens_ref.1) | copy-start | bytes 2211844
  3.7 0.7 copy-start.2
  4.4 0.7 copy-start.3
  5.1 0.7 copy-start.4
  5.7 0.7 copy-start.5

commit v3 on v2

--- a/solution.py
+++ b/solution.py
@@ -21,7 +21,6 @@
 QUERY_CUTS = 3
 OUT_CUTS = 3
 HOP_CUTS = 3
-EARLY = 4
 
 
 def rotary(positions, head_size):
@@ -202,42 +201,7 @@
             def _():
                 w_copy(t, off, 1).start()
 
-    @pl.when(sec == 0)
-    def _():
-        @pl.loop(0, micro)
-        def _(t):
-            enter(t)
-
-    def source(d, which):
-        return ((chip - d + chips) % chips) * 2 + which
-
-    def relay_y(kind, k, d):
-        for e in range(1, groups):
-            y_copy(kind, d, k, e, source(d, core), (g - e + groups) % groups).wait_recv()
-            d_copy(kind, d, k, e, source(d, core)).start()
-
-    previous = None
-    for kind, k, d in plan:
-        x_copy(kind, d, k, source(d, core)).wait_recv()
-        for e in range(1, groups):
-            y_copy(kind, d, k, e, source(d, core), g).start()
-        d_copy(kind, d, k, 0, source(d, core)).start()
-        if previous is not None:
-            relay_y(*previous)
-        previous = (kind, k, d)
-    if previous is not None:
-        relay_y(*previous)
-    for kind in range(2):
-        own_copy(kind, partner).wait_recv()
-    for kind, k, d in plan:
-        for e in range(groups):
-            d_copy(kind, d, k, e, source(d, 1 - core)).wait_recv()
-
-    def slot(t, carry):
-        @pl.when(sec > 0)
-        def _():
-            enter(t)
-
+    def attend(t, heads):
         length = length_ref[order_ref[t]]
         normed = normed_ref[t]
 
@@ -248,16 +212,16 @@
                 qbuf[:, s * shard + p * LANES:s * shard + (p + 1) * LANES] = rotated.astype(BF16)
 
         per_head = seq // kv_heads
-        early = min(EARLY, kv_heads)
-        for s in range(early * per_head):
+        for s in range(heads[0] * per_head, (heads[-1] + 1) * per_head):
             ask(s)
 
-        for off in range(1, depth + 1):
-
-            @pl.when(q >= off)
-            def _():
-                w_copy(t, off, 0).wait_recv()
-                w_copy(t, off, 1).wait_recv()
+        if heads[0] == 0:
+            for off in range(1, depth + 1):
+
+                @pl.when(q >= off)
+                def _():
+                    w_copy(t, off, 0).wait_recv()
+                    w_copy(t, off, 1).wait_recv()
 
         span = WIN + rows
         row = lax.broadcasted_iota(jnp.int32, (rows, span), 0)
@@ -307,14 +271,64 @@
                 context = context / jnp.where(low, sides[0][1], sides[1][1])
                 cbuf[:, at:at + LANES] = context.astype(BF16)
 
-        scores = score(0)
-        for h in range(kv_heads):
-            following = score(h + 1) if h + 1 < kv_heads else None
-            if h + early < kv_heads:
-                for s in range((h + early) * per_head, (h + early + 1) * per_head):
-                    ask(s)
+        scores = score(heads[0])
+        for h in heads:
+            following = score(h + 1) if h + 1 in heads else None
             mix(h, scores)
             scores = following
+
+    @pl.when(sec == 0)
+    def _():
+        @pl.loop(0, micro)
+        def _(t):
+            enter(t)
+
+    def source(d, which):
+        return ((chip - d + chips) % chips) * 2 + which
+
+    def relay_y(kind, k, d):
+        for e in range(1, groups):
+            y_copy(kind, d, k, e, source(d, core), (g - e + groups) % groups).wait_recv()
+            d_copy(kind, d, k, e, source(d, core)).start()
+
+    previous = None
+    for kind, k, d in plan:
+        x_copy(kind, d, k, source(d, core)).wait_recv()
+        for e in range(1, groups):
+            y_copy(kind, d, k, e, source(d, core), g).start()
+        d_copy(kind, d, k, 0, source(d, core)).start()
+        if previous is not None:
+            relay_y(*previous)
+        previous = (kind, k, d)
+        if kind == 1 and d == 1 and k == 1:
+            own_copy(0, partner).wait_recv()
+            for one in plan:
+                if one[0] == 0:
+                    for e in range(groups):
+                        d_copy(*one[:1], one[2], one[1], e, source(one[2], 1 - core)).wait_recv()
+        if kind == 1 and d == 1 and k >= 1:
+            share = kv_heads // 2
+
+            @pl.when(sec == 0)
+            def _():
+                attend(0, tuple(range((k - 1) * share, k * share)))
+
+    if previous is not None:
+        relay_y(*previous)
+    own_copy(1, partner).wait_recv()
+    for kind, k, d in plan:
+        for e in range(groups if kind else 0):
+            d_copy(kind, d, k, e, source(d, 1 - core)).wait_recv()
+
+    def slot(t, carry):
+        @pl.when(sec > 0)
+        def _():
+            enter(t)
+
+        @pl.when((sec > 0) | (t > 0))
+        def _():
+            attend(t, tuple(range(kv_heads)))
+
         for c, (first, size) in enumerate(edges):
             output = lax.dot_general(
                 cbuf[...], out_w[first:first + size], (((1,), (1,)), ((), ())),

time: 106 us -> 106 us (level)
  no operation moved by 1% of the time
where the time goes in v3:
time: 106 us
  Pallas kernels  97.5 us (92%)
  local copies, waits for them, and re-layouts  7 us (7%)
    pallas_call x1, Pallas kernels, per_device(): pl.pallas_call(functools.partial(kernel, shape), out_shape=(jax.ShapeDtyp...  97.5 us
    unnamed x14, local copies, waits for them, and re-layouts  6.75 us

profile of v3, /device:TPU:27, one launch (start us, length us, event | category | flops | bytes accessed | tf_op | source)
XLA Modules:
  0.0 105.5 jit_solution(5847665565379801713)
XLA Ops:
  0.7 0.2 fusion
  0.9 0.1 pad_maximum_fusion
  1.0 0.1 tile.9.cos_ref
  1.1 0.1 tile.21.sin_ref
  1.2 0.0 copy-start
  1.2 1.4 %copy-done = bf16[1,1440,512]{2,1,0:T(8,128)(2,1)S(1)} copy-done((bf16[1,1440,512]{2,1,0:T(8,128)(2,1)S(1)}, bf16[1,1440,512]{2,1,0:T(8,128)(2,1)}, u32[]{:S(2)}) %copy-start) | copy-done | bytes 1474584
  2.6 0.0 copy-start.1
  2.6 1.1 %copy-done.1 = bf16[4,64,1440]{2,1,0:T(8,128)(2,1)S(1)} copy-done((bf16[4,64,1440]{2,1,0:T(8,128)(2,1)S(1)}, bf16[4,64,1440]{2,1,0:T(8,128)(2,1)}, u32[]{:S(2)}) %copy-start.1) | copy-done | bytes 737304
  3.7 0.0 copy-start.2
  3.7 0.7 copy-done.2
  4.4 0.0 copy-start.3
  4.4 0.7 copy-done.3
  5.1 0.0 copy-start.4
  5.1 0.7 copy-done.4
  5.7 0.0 copy-start.5
  5.7 0.7 copy-done.5
  6.4 97.5 %shard_map.95 = (bf16[4,64,1440]{2,1,0:T(8,128)(2,1)S(1)}, bf16[4,64,512]{2,1,0:T(8,128)(2,1)S(1)}) custom-call(s32[4]{0:T(128)S(1)} %copy-done.3, s32[4]{0:T(128)S(1)} %copy-done.4, f32[32]{0:T(128)S(1)} %bitcast.11, bf16[4,64,1440]{2,1,0:T(8,128)(2,1)S(1)} %copy-done.1, f32[1,1440]{1,0:T(1,128)S(1)} %copy-done.2, f32[64,128]{1,0:T(8,128)S(1)} %tile.9.cos_ref, ...), custom_call_target="tpu_custom_call" | custom-call | tf_op jit(solution)/shard_map/pallas_call | solution.py:391
  103.9 0.9 copy.12
  104.8 0.7 copy.13
  (4 shorter events, 0.1 us)
Async XLA Ops:
  1.2 1.4 %copy-start = (bf16[1,1440,512]{2,1,0:T(8,128)(2,1)S(1)}, bf16[1,1440,512]{2,1,0:T(8,128)(2,1)}, u32[]{:S(2)}) copy-start(bf16[1,1440,512]{2,1,0:T(8,128)(2,1)} %param.13) | copy-start | bytes 4423684
  2.6 1.1 %copy-start.1 = (bf16[4,64,1440]{2,1,0:T(8,128)(2,1)S(1)}, bf16[4,64,1440]{2,1,0:T(8,128)(2,1)}, u32[]{:S(2)}) copy-start(bf16[4,64,1440]{2,1,0:T(8,128)(2,1)} %tokens_ref.1) | copy-start | bytes 2211844
  3.7 0.7 copy-start.2
  4.4 0.7 copy-start.3
  5.1 0.7 copy-start.4
  5.7 0.7 copy-start.5
